TPU v7x, 32 devices: a whole 2x2x4 slice. The times are simulated.
32 devices in a mesh: rep: 1, r: 8 (over y, z), s: 4 (over x, core).
Axes of the slice: x: 2, y: 2, z: 4, core: 2. Of those that a mesh axis runs over, the one named last changes fastest.
Arguments:
- x: bfloat16 [32, 4096, 896], P(('rep', 'r', 's'))
- dy: bfloat16 [32, 4096, 896], P(('rep', 'r', 's'))
- w_gate: bfloat16 [2, 896, 2304], P(None, 's')
- w_up: bfloat16 [2, 896, 2304], P(None, 's')
- w_down: bfloat16 [2, 2304, 896], P(None, 's')
- m_w_gate: float32 [2, 896, 2304], P(None, 's')
- m_w_up: float32 [2, 896, 2304], P(None, 's')
- m_w_down: float32 [2, 2304, 896], P(None, 's')
- v_w_gate: float32 [2, 896, 2304], P(None, 's')
- v_w_up: float32 [2, 896, 2304], P(None, 's')
- v_w_down: float32 [2, 2304, 896], P(None, 's')
Outputs:
- output 1: bfloat16 [2, 896, 2304], P('rep', 's')
- output 2: bfloat16 [2, 896, 2304], P('rep', 's')
- output 3: bfloat16 [2, 2304, 896], P('rep', 's')
- output 4: float32 [2, 896, 2304], P('rep', 's')
- output 5: float32 [2, 896, 2304], P('rep', 's')
- output 6: float32 [2, 2304, 896], P('rep', 's')
- output 7: float32 [2, 896, 2304], P('rep', 's')
- output 8: float32 [2, 896, 2304], P('rep', 's')
- output 9: float32 [2, 2304, 896], P('rep', 's')
All inputs are finite; a program needn't handle non-finite values.
Results may differ from a plain program's by a relative error of at most 0.022.
Values are sent between devices in bfloat16 or wider.
A program may use at most 2 GiB of HBM per device.

v0:
```python
import jax
import jax.numpy as jnp
from jax import lax
from jax.sharding import PartitionSpec as P

NAMES = ("w_gate", "w_up", "w_down")


def matmul(a, w):
    return jnp.dot(a, w, preferred_element_type=jnp.float32).astype(jnp.bfloat16)


def normed(h):
    wide = h.astype(jnp.float32)
    scale = lax.rsqrt(jnp.mean(wide**2, -1, keepdims=True) + 1e-6)
    return (wide * scale).astype(jnp.bfloat16)


def layer(h, w):
    a = normed(h)
    gate = jnp.dot(a, w["w_gate"], preferred_element_type=jnp.float32)
    up = jnp.dot(a, w["w_up"], preferred_element_type=jnp.float32)
    return h + matmul((jax.nn.silu(gate) * up).astype(jnp.bfloat16), w["w_down"])


def adamw(w, m, v, g):
    m = 0.9 * m + 0.1 * g
    v = 0.95 * v + 0.05 * g * g
    step = m * lax.rsqrt(v + 1e-8) + 0.1 * w
    return (w - 0.02 * step).astype(jnp.bfloat16), m, v


def clipped(gradients, sum_of_squares, count):
    factor = jnp.minimum(1.0, 0.5 * lax.rsqrt(sum_of_squares / count + 1e-30))
    return [g * factor for g in gradients]


def solution(mesh):
    def fetched(weights, number):
        return {name: lax.all_gather(w[number], "s", axis=0, tiled=True) for name, w in zip(NAMES, weights, strict=True)}

    def summed(term):
        return lax.psum(lax.psum_scatter(term, "s", scatter_dimension=0, tiled=True), "r")

    def step(x, dy, *arrays):
        weights, m, v = (arrays[i : i + 3] for i in (0, 3, 6))
        layers = weights[0].shape[0]
        h, kept = x[0], []
        for number in range(layers):
            kept.append(h)
            h = layer(h, fetched(weights, number))
        by_h, mine = dy[0], [None] * layers
        for number in reversed(range(layers)):
            _, back = jax.vjp(lambda w, h: layer(h, w), fetched(weights, number), kept[number])
            by_w, by_h = back(by_h)
            mine[number] = [summed(by_w[name]) for name in NAMES]
        gradients = [jnp.stack([mine[number][i] for number in range(layers)]).astype(jnp.float32) for i in range(3)]
        squares = lax.psum(sum(jnp.sum(g * g) for g in gradients), "s")
        gradients = clipped(gradients, squares, lax.psum(1, "s") * sum(g.size for g in gradients))
        new = [adamw(w.astype(jnp.float32), m, v, g) for w, m, v, g in zip(weights, m, v, gradients, strict=True)]
        return tuple(one[which] for which in range(3) for one in new)

    states, cut = P(("rep", "r", "s"), None, None), P(None, "s", None)
    return jax.shard_map(
        step,
        mesh=mesh,
        in_specs=(states, states) + (cut,) * 9,
        out_specs=(P("rep", "s", None),) * 9,
        check_vma=False,
    )
```

profile of v0, /device:TPU:0, one launch (start us, length us, event | category | flops | bytes accessed | tf_op | source)
XLA Modules:
  0.0 914.5 jit_solution(2110221617210943143)
XLA Ops:
  7.2 0.0 all-gather.13.cloned.1.call-start
  7.2 3.1 fusion.91
  10.4 0.0 all-gather.15.cloned.1.call-start
  10.4 3.0 fusion.90
  13.4 0.0 all-gather.17.cloned.1.call-start
  13.5 1.5 fusion.89
  15.0 0.0 all-gather.23.cloned.1.call-start
  15.0 0.5 all-gather.23.cloned.1.call-update
  15.5 0.0 all-gather.21.cloned.1.call-start
  15.6 0.5 all-gather.21.cloned.1.call-update
  16.1 0.0 all-gather.19.cloned.1.call-start
  16.2 0.5 all-gather.19.cloned.1.call-update
  16.7 0.0 reduce-scatter.15.cloned.1.call-start
  16.7 10.8 %copy.20 = bf16[1,4096,896]{1,2,0:T(8,128)(2,1)} copy(bf16[1,4096,896]{2,1,0:T(8,128)(2,1)} %param.11) | data formatting | bytes 14680064 | tf_op args[0]
  27.5 4.6 fusion.15
  32.1 10.7 %copy.21 = bf16[1,4096,896]{1,2,0:T(8,128)(2,1)} copy(bf16[1,4096,896]{2,1,0:T(8,128)(2,1)} %param.12) | data formatting | bytes 14680064 | tf_op args[1]
  42.9 4.3 all-gather.13.cloned.1.call-done
  47.2 27.0 %fusion.47 = f32[4096,2304]{1,0:T(8,128)} fusion(bf16[1,4096,896]{1,2,0:T(8,128)(2,1)} %copy.20, f32[4096]{0:T(1024)S(1)} %add_rsqrt_fusion, bf16[1,896,2304]{2,1,0:T(8,128)(2,1)} %all-gather.13.cloned.1.call-done), kind=kOutput, calls=%fused_computation.72 | convolution fusion | flops 16922443776 | bytes 49233920 | tf_op jit(solution)/shard_map/dot_general | solution.py:21
  74.2 9.1 all-gather.15.cloned.1.call-done
  83.3 41.9 %multiply_convert_fusion.1 = (bf16[4096,2304]{1,0:T(8,128)(2,1)}, f32[4096,2304]{1,0:T(8,128)}) fusion(f32[4096,2304]{1,0:T(8,128)} %fusion.47, bf16[1,896,2304]{2,1,0:T(8,128)(2,1)} %all-gather.15.cloned.1.call-done, bf16[1,4096,896]{1,2,0:T(8,128)(2,1)} %copy.20, f32[4096]{0:T(1024)S(1)} %add_rsqrt_fusion), kind=kOutput, calls=%fused_computation.17 | convolution fusion | flops 16979066880 | bytes 105857024 | tf_op jit(solution)/shard_map/dot_general | solution.py:22
  125.2 24.4 %fusion.19 = (f32[4096]{0:T(1024)S(1)}, bf16[4096,896]{0,1:T(8,128)(2,1)}) fusion(bf16[4096,2304]{1,0:T(8,128)(2,1)} %get-tuple-element.30, bf16[1,2304,896]{2,1,0:T(8,128)(2,1)} %all-gather.17.cloned.1.call-done, bf16[1,4096,896]{1,2,0:T(8,128)(2,1)} %copy.20), kind=kOutput, calls=%fused_computation.37 | convolution fusion | flops 16929779712 | bytes 37699584 | tf_op jit(solution)/shard_map/dot_general | solution.py:10
  149.6 0.6 copy-done.13
  150.2 5.0 all-gather.23.cloned.1.call-done
  155.3 27.0 %fusion.39 = f32[4096,2304]{1,0:T(8,128)} fusion(bf16[4096,896]{0,1:T(8,128)(2,1)} %get-tuple-element.33, f32[4096]{0:T(1024)S(1)} %fusion.77, bf16[1,896,2304]{2,1,0:T(8,128)(2,1)} %all-gather.23.cloned.1.call-done), kind=kOutput, calls=%fused_computation.69 | convolution fusion | flops 16922443776 | bytes 49233920 | tf_op jit(solution)/shard_map/jvp()/dot_general | solution.py:22
  182.3 8.9 all-gather.21.cloned.1.call-done
  191.2 26.5 %convolution_convert_fusion.1 = bf16[4096,2304]{1,0:T(8,128)(2,1)} fusion(bf16[1,4096,896]{2,1,0:T(8,128)(2,1)} %param.12, bf16[1,2304,896]{2,1,0:T(8,128)(2,1)} %all-gather.21.cloned.1.call-done), kind=kOutput, calls=%fused_computation.27 | convolution fusion | flops 16920870912 | bytes 30343168 | tf_op jit(solution)/shard_map/transpose(jvp())/dot_general | solution.py:10
  217.7 9.4 %all-gather.19.cloned.1.call-done = bf16[1,896,2304]{2,1,0:T(8,128)(2,1)} async-done(((bf16[1,224,2304]{2,1,0:T(8,128)(2,1)}), bf16[1,896,2304]{2,1,0:T(8,128)(2,1)}) %all-gather.19.cloned.1.call-update) | async-done | bytes 4128784 | tf_op jit(solution)/shard_map/all_gather | solution.py:40
  227.1 52.3 %fusion.2 = (bf16[4096,2304]{1,0:T(8,128)(2,1)}, f32[4096,2304]{1,0:T(8,128)}) fusion(f32[4096,2304]{1,0:T(8,128)} %fusion.39, bf16[4096,2304]{1,0:T(8,128)(2,1)} %convolution_convert_fusion.1, bf16[1,896,2304]{2,1,0:T(8,128)(2,1)} %all-gather.19.cloned.1.call-done, bf16[4096,896]{0,1:T(8,128)(2,1)} %get-tuple-element.33, f32[4096]{0:T(1024)S(1)} %fusion.77), kind=kOutput, calls=%fused_computation.8 | convolution fusion | flops 17035689984 | bytes 124731392 | tf_op jit(solution)/shard_map/jvp()/dot_general | solution.py:21
  279.4 22.8 %fusion.70 = bf16[4096,896]{0,1:T(8,128)(2,1)} fusion(bf16[4096,2304]{1,0:T(8,128)(2,1)} %get-tuple-element.34, bf16[1,896,2304]{2,1,0:T(8,128)(2,1)} %all-gather.19.cloned.1.call-done), kind=kOutput, calls=%fused_computation.94 | convolution fusion | flops 16911433728 | bytes 30343168 | tf_op jit(solution)/shard_map/transpose(jvp())/dot_general | solution.py:21
  302.2 35.3 %fusion.21 = (f32[4096]{0:T(1024)S(1)}, bf16[4096,896]{0,1:T(8,128)(2,1)}) fusion(bf16[4096,896]{0,1:T(8,128)(2,1)} %get-tuple-element.33, bf16[4096,896]{0,1:T(8,128)(2,1)} %fusion.70, bf16[1,896,2304]{2,1,0:T(8,128)(2,1)} %all-gather.23.cloned.1.call-done, bf16[4096,2304]{1,0:T(8,128)(2,1)} %convolution_convert_fusion.1, f32[4096,2304]{1,0:T(8,128)} %get-tuple-element.35), kind=kOutput, calls=%fused_computation.39 | convolution fusion | flops 16990072832 | bytes 82788352 | tf_op jit(solution)/shard_map/transpose(jvp())/dot_general | solution.py:22
  337.5 9.8 %fusion.22 = bf16[4096,896]{0,1:T(8,128)(2,1)S(1)} fusion(bf16[4096,896]{0,1:T(8,128)(2,1)} %get-tuple-element.33, bf16[4096,896]{0,1:T(8,128)(2,1)} %get-tuple-element.37, bf16[1,4096,896]{1,2,0:T(8,128)(2,1)} %copy.21, f32[4096]{0:T(1024)S(1)} %multiply_multiply_fusion.3, f32[4096]{0:T(1024)S(1)} %fusion.77), kind=kLoop, calls=%fused_computation.40 | loop fusion | flops 25690112 | bytes 29392896 | tf_op jit(solution)/shard_map/transpose(jvp())/add_any | solution.py:14
  347.3 2.9 copy-done.4
  350.2 24.2 %convolution_convert_fusion.2 = bf16[2304,896]{1,0:T(8,128)(2,1)} fusion(bf16[4096,2304]{1,0:T(8,128)(2,1)} %get-tuple-element.30, bf16[4096,896]{0,1:T(8,128)(2,1)S(1)} %fusion.22), kind=kOutput, calls=%fused_computation.52 | convolution fusion | flops 16913498112 | bytes 30343168 | tf_op jit(solution)/shard_map/transpose(jvp())/dot_general | solution.py:10
  374.5 0.0 reduce-scatter.17.cloned.1.call-start
  374.5 34.1 %fusion.26 = bf16[2304,896]{1,0:T(8,128)(2,1)} fusion(bf16[1,4096,896]{2,1,0:T(8,128)(2,1)} %param.12, f32[4096,2304]{1,0:T(8,128)} %fusion.39, f32[4096,2304]{1,0:T(8,128)} %get-tuple-element.35), kind=kOutput, calls=%fused_computation.48 | convolution fusion | flops 16970121216 | bytes 86966272 | tf_op jit(solution)/shard_map/transpose(jvp())/dot_general | solution.py:10
  408.6 0.0 reduce-scatter.11.cloned.1.call-start
  408.7 27.4 %convolution_convert_fusion = bf16[4096,2304]{1,0:T(8,128)(2,1)} fusion(bf16[4096,896]{0,1:T(8,128)(2,1)} %copy-done.4, bf16[1,2304,896]{2,1,0:T(8,128)(2,1)} %all-gather.17.cloned.1.call-done), kind=kOutput, calls=%fused_computation.26 | convolution fusion | flops 16920870912 | bytes 30343168 | tf_op jit(solution)/shard_map/transpose(jvp())/dot_general | solution.py:10
  436.1 34.5 %fusion.33 = bf16[896,2304]{1,0:T(8,128)(2,1)} fusion(bf16[4096,2304]{1,0:T(8,128)(2,1)} %convolution_convert_fusion, f32[4096,2304]{1,0:T(8,128)} %fusion.47, bf16[1,4096,896]{1,2,0:T(8,128)(2,1)} %copy.20, f32[4096]{0:T(1024)S(1)} %copy-done.16), kind=kOutput, calls=%fused_computation.51 | convolution fusion | flops 16981131264 | bytes 68108288 | tf_op jit(solution)/shard_map/transpose(jvp())/dot_general | solution.py:22
  470.6 0.0 reduce-scatter.13.cloned.1.call-start
  470.6 34.1 %fusion.29 = bf16[896,2304]{1,0:T(8,128)(2,1)} fusion(bf16[4096,2304]{1,0:T(8,128)(2,1)} %convolution_convert_fusion.1, bf16[4096,896]{0,1:T(8,128)(2,1)} %get-tuple-element.33, f32[4096]{0:T(1024)S(1)} %copy-done.12, f32[4096,2304]{1,0:T(8,128)} %get-tuple-element.35), kind=kOutput, calls=%fused_computation.49 | convolution fusion | flops 16981131264 | bytes 68108288 | tf_op jit(solution)/shard_map/transpose(jvp())/dot_general | solution.py:22
  504.7 0.0 reduce-scatter.7.cloned.1.call-start
  504.8 39.4 %fusion.30 = bf16[896,2304]{1,0:T(8,128)(2,1)} fusion(f32[4096,2304]{1,0:T(8,128)} %fusion.47, f32[4096,2304]{1,0:T(8,128)} %get-tuple-element.31, bf16[4096,2304]{1,0:T(8,128)(2,1)} %convolution_convert_fusion, bf16[1,4096,896]{1,2,0:T(8,128)(2,1)} %copy.20, f32[4096]{0:T(1024)S(1)} %copy-done.16), kind=kOutput, calls=%fused_computation.50 | convolution fusion | flops 17028317184 | bytes 105857024 | tf_op jit(solution)/shard_map/transpose(jvp())/dot_general | solution.py:21
  544.1 0.0 reduce-scatter.9.cloned.1.call-start
  544.2 23.8 %convolution_convert_fusion.3 = bf16[896,2304]{1,0:T(8,128)(2,1)} fusion(bf16[4096,2304]{1,0:T(8,128)(2,1)} %get-tuple-element.34, bf16[4096,896]{0,1:T(8,128)(2,1)} %get-tuple-element.33, f32[4096]{0:T(1024)S(1)} %copy-done.12), kind=kOutput, calls=%fused_computation.53 | convolution fusion | flops 16922443776 | bytes 30359552 | tf_op jit(solution)/shard_map/transpose(jvp())/dot_general | solution.py:21
  568.0 0.0 all-reduce.3.cloned.1.call-start
  568.1 0.0 reduce-scatter.15.cloned.1.call-done
  568.1 0.0 reduce-scatter.17.cloned.1.call-done
  568.1 0.0 reduce-scatter.11.cloned.1.call-done
  568.1 0.0 reduce-scatter.13.cloned.1.call-done
  568.2 39.0 %reduce-scatter.7.cloned.1.call-done = bf16[224,2304]{1,0:T(8,128)(2,1)} async-done(((bf16[896,2304]{1,0:T(8,128)(2,1)}), bf16[224,2304]{1,0:T(8,128)(2,1)}) %reduce-scatter.7.cloned.1.call-update) | async-done | bytes 1032208 | tf_op jit(solution)/shard_map/reduce_scatter | solution.py:43
  607.2 46.5 %reduce-scatter.9.cloned.1.call-done = bf16[224,2304]{1,0:T(8,128)(2,1)} async-done(((bf16[896,2304]{1,0:T(8,128)(2,1)}), bf16[224,2304]{1,0:T(8,128)(2,1)}) %reduce-scatter.9.cloned.1.call-update) | async-done | bytes 1032208 | tf_op jit(solution)/shard_map/reduce_scatter | solution.py:43
  653.7 212.5 %all-reduce.3.cloned.1.call-done = (bf16[1,224,2304]{2,1,0:T(8,128)(2,1)}, bf16[1,224,2304]{2,1,0:T(8,128)(2,1)}, bf16[1,224,2304]{2,1,0:T(8,128)(2,1)}, bf16[1,...) async-done(((bf16[1,224,2304]{2,1,0:T(8,128)(2,1)}, bf16[1,224,2304]{2,1,0:T(8,128)(2,1)}, bf16[1,224,2304]{2,1,0:T(8,128)(2,1)}, ...) | async-done | bytes 6193168 | tf_op jit(solution)/shard_map/psum | solution.py:43
  866.2 3.2 fusion.57
  869.4 3.2 fusion.56
  872.6 3.2 fusion.55
  877.8 6.3 psum.55
  884.9 9.0 fusion.63
  893.9 0.9 copy-done.5
  894.8 1.2 copy-done.6
  896.0 1.2 copy-done.7
  897.2 1.2 copy-done.8
  898.4 0.2 copy-done.9
  898.6 0.3 copy-done.10
  898.9 8.9 fusion.54
  (40 shorter events, 0.3 us)
Async XLA Ops:
  7.2 6.3 copy-start
  7.2 40.0 %all-gather.13.cloned.1.call-start = ((), (), s32[]{:S(2)}) async-start(), calls=%async_computation.12 | async-start | bytes 5160960 | tf_op jit(solution)/shard_map/all_gather | solution.py:40
  10.4 72.9 %all-gather.15.cloned.1.call-start = ((), (), s32[]{:S(2)}) async-start(), calls=%async_computation.13 | async-start | bytes 5160960 | tf_op jit(solution)/shard_map/all_gather | solution.py:40
  13.4 111.8 %all-gather.17.cloned.1.call-start = ((), (), s32[]{:S(2)}) async-start(), calls=%async_computation.14 | async-start | bytes 5160960 | tf_op jit(solution)/shard_map/all_gather | solution.py:40
  15.0 140.3 %all-gather.23.cloned.1.call-start = ((), (), s32[]{:S(2)}) async-start(), calls=%async_computation.17 | async-start | bytes 5160960 | tf_op jit(solution)/shard_map/all_gather | solution.py:40
  15.5 175.7 %all-gather.21.cloned.1.call-start = ((), (), s32[]{:S(2)}) async-start(), calls=%async_computation.16 | async-start | bytes 5160960 | tf_op jit(solution)/shard_map/all_gather | solution.py:40
  16.1 211.0 %all-gather.19.cloned.1.call-start = ((), (), s32[]{:S(2)}) async-start(), calls=%async_computation.15 | async-start | bytes 5160960 | tf_op jit(solution)/shard_map/all_gather | solution.py:40
  16.7 551.4 %reduce-scatter.15.cloned.1.call-start = ((), (), s32[]{:S(2)}) async-start(), calls=%async_computation.10 | async-start | bytes 5160960 | tf_op jit(solution)/shard_map/reduce_scatter | solution.py:43
  32.1 51.1 %copy-start.15 = (f32[4096]{0:T(1024)}, f32[4096]{0:T(1024)S(1)}, u32[]{:S(2)}) copy-start(f32[4096]{0:T(1024)S(1)} %add_rsqrt_fusion) | copy-start | bytes 49156
  149.6 0.6 copy-start.13
  150.2 187.3 %copy-start.11 = (f32[4096]{0:T(1024)}, f32[4096]{0:T(1024)S(1)}, u32[]{:S(2)}) copy-start(f32[4096]{0:T(1024)S(1)} %fusion.77) | copy-start | bytes 49156
  302.2 35.3 %copy-start.14 = (f32[4096]{0:T(1024)S(1)}, f32[4096]{0:T(1024)}, u32[]{:S(2)}) copy-start(f32[4096]{0:T(1024)} %copy-done.13) | copy-start | bytes 49156
  347.3 2.9 copy-start.4
  374.5 193.6 %reduce-scatter.17.cloned.1.call-start = ((), (), s32[]{:S(2)}) async-start(), calls=%async_computation.11 | async-start | bytes 5160960 | tf_op jit(solution)/shard_map/reduce_scatter | solution.py:43
  408.6 27.5 %copy-start.16 = (f32[4096]{0:T(1024)S(1)}, f32[4096]{0:T(1024)}, u32[]{:S(2)}) copy-start(f32[4096]{0:T(1024)} %copy-done.15) | copy-start | bytes 49156
  408.6 159.5 %reduce-scatter.11.cloned.1.call-start = ((), (), s32[]{:S(2)}) async-start(), calls=%async_computation.8 | async-start | bytes 5160960 | tf_op jit(solution)/shard_map/reduce_scatter | solution.py:43
  436.1 34.5 %copy-start.12 = (f32[4096]{0:T(1024)S(1)}, f32[4096]{0:T(1024)}, u32[]{:S(2)}) copy-start(f32[4096]{0:T(1024)} %copy-done.11) | copy-start | bytes 49156
  470.6 97.6 %reduce-scatter.13.cloned.1.call-start = ((), (), s32[]{:S(2)}) async-start(), calls=%async_computation.9 | async-start | bytes 5160960 | tf_op jit(solution)/shard_map/reduce_scatter | solution.py:43
  504.7 102.5 %reduce-scatter.7.cloned.1.call-start = ((), (), s32[]{:S(2)}) async-start(), calls=%async_computation.6 | async-start | bytes 5160960 | tf_op jit(solution)/shard_map/reduce_scatter | solution.py:43
  544.1 109.5 %reduce-scatter.9.cloned.1.call-start = ((), (), s32[]{:S(2)}) async-start(), calls=%async_computation.7 | async-start | bytes 5160960 | tf_op jit(solution)/shard_map/reduce_scatter | solution.py:43
  568.0 316.8 %copy-start.1 = (bf16[2,576,896]{2,1,0:T(8,128)(2,1)S(1)}, bf16[2,576,896]{2,1,0:T(8,128)(2,1)}, u32[]{:S(2)}) copy-start(bf16[2,576,896]{2,1,0:T(8,128)(2,1)} %param.15) | copy-start | bytes 6193156
  568.0 298.2 %all-reduce.3.cloned.1.call-start = ((), (), s32[]{:S(2)}) async-start(), calls=%async_computation.18 | async-start | bytes 12386304 | tf_op jit(solution)/shard_map/psum | solution.py:43
  884.8 9.1 copy-start.2
  884.8 9.0 copy-start.3
  884.9 10.0 %copy-start.5 = (f32[2,224,2304]{2,1,0:T(8,128)S(1)}, f32[2,224,2304]{2,1,0:T(8,128)}, u32[]{:S(2)}) copy-start(f32[2,224,2304]{2,1,0:T(8,128)} %param.19) | copy-start | bytes 12386308
  884.9 11.2 %copy-start.6 = (f32[2,224,2304]{2,1,0:T(8,128)S(1)}, f32[2,224,2304]{2,1,0:T(8,128)}, u32[]{:S(2)}) copy-start(f32[2,224,2304]{2,1,0:T(8,128)} %param.16) | copy-start | bytes 12386308
  884.9 12.3 %copy-start.7 = (f32[2,224,2304]{2,1,0:T(8,128)S(1)}, f32[2,224,2304]{2,1,0:T(8,128)}, u32[]{:S(2)}) copy-start(f32[2,224,2304]{2,1,0:T(8,128)} %param.20) | copy-start | bytes 12386308
  884.9 13.5 %copy-start.8 = (f32[2,224,2304]{2,1,0:T(8,128)S(1)}, f32[2,224,2304]{2,1,0:T(8,128)}, u32[]{:S(2)}) copy-start(f32[2,224,2304]{2,1,0:T(8,128)} %param.17) | copy-start | bytes 12386308
  884.9 13.7 %copy-start.9 = (bf16[1,224,2304]{2,1,0:T(8,128)(2,1)S(1)}, bf16[1,224,2304]{2,1,0:T(8,128)(2,1)}, u32[]{:S(2)}) copy-start(bf16[1,224,2304]{2,1,0:T(8,128)(2,1)} %get-tuple-element.9) | copy-start | bytes 3096580
  884.9 14.0 %copy-start.10 = (bf16[1,224,2304]{2,1,0:T(8,128)(2,1)S(1)}, bf16[1,224,2304]{2,1,0:T(8,128)(2,1)}, u32[]{:S(2)}) copy-start(bf16[1,224,2304]{2,1,0:T(8,128)(2,1)} %get-tuple-element.10) | copy-start | bytes 3096580
Sparse Core Ops, SparseCore 0:
  10.5 36.6 all-gather.12
  49.3 33.8 all-gather.14
  85.4 33.9 all-gather.16
  121.3 33.8 all-gather.22
  157.2 33.8 all-gather.20
  193.2 33.8 all-gather.18
  374.6 43.4 reduce-scatter.14
  421.2 43.4 reduce-scatter.16
  470.7 43.4 reduce-scatter.10
  517.1 43.4 reduce-scatter.12
  563.8 43.4 reduce-scatter.6
  610.2 43.4 reduce-scatter.8
  658.8 207.3 all-reduce.2
where the time goes:
time: 921 us; the launch traced here: 915 us
  matrix products  475 us (52%)
  waiting for transfers between devices  337 us (37%)
  other arithmetic  41.8 us (5%)
  local copies, waits for them, and re-layouts  37.7 us (4%)
  between operations  17 us (2%)
    psum x1, waiting for transfers between devices, summed(): lax.psum(lax.psum_scatter(term, 's', scatter_dimension=0, tiled=True), 'r')  213 us
    dot_general x5, matrix products, layer(): up = jnp.dot(a, w['w_up'], preferred_element_type=jnp.float32)  173 us
    dot_general x5, matrix products, layer(): gate = jnp.dot(a, w['w_gate'], preferred_element_type=jnp.float32)  165 us
    dot_general x5, matrix products, matmul(): jnp.dot(a, w, preferred_element_type=jnp.float32).astype(jnp.bfloat16)  137 us
    reduce_scatter x6, waiting for transfers between devices, summed(): lax.psum_scatter(term, 's', scatter_dimension=0, tiled=True)  85.6 us
    all_gather x6, waiting for transfers between devices, fetched(): lax.all_gather(w[number], 's', axis=0, tiled=True)  36.7 us
    unnamed x36, local copies, waits for them, and re-layouts  30.1 us
  transfers between devices with their start and end apart: 13, of which 8 were waited for; matrix products, arithmetic and copies ran while one was open for 41% of the time, Pallas kernels for 0%

commit v1 on v0

v1 whole, which is shorter than its diff:
```python
import functools

import jax
import jax.numpy as jnp
from jax import lax
from jax.experimental import pallas as pl
from jax.experimental.pallas import tpu as pltpu
from jax.sharding import PartitionSpec as P

bf16, f32 = jnp.bfloat16, jnp.float32
MESH = pl.DeviceIdType.MESH
MIB = 2**20


def nn(a, b):
    return jnp.dot(a, b, preferred_element_type=f32)


def nt(a, b):
    return lax.dot_general(a, b, (((1,), (1,)), ((), ())), preferred_element_type=f32)


def tn(a, b):
    return lax.dot_general(a, b, (((0,), (0,)), ((), ())), preferred_element_type=f32)


def normed(h):
    wide = h.astype(f32)
    scale = lax.rsqrt(jnp.mean(wide * wide, -1, keepdims=True) + 1e-6)
    return wide, scale, (wide * scale).astype(bf16)


def backward(dact, gate, up):
    sig = lax.logistic(gate)
    silu = gate * sig
    return silu, dact * up * (sig + silu * (1.0 - sig)), dact * silu


def spread(act_ref, k, act):
    for e in range(4):
        block, third = divmod(4 * k + e, 3)
        act_ref[:, 768 * third + 192 * block : 768 * third + 192 * (block + 1)] = act[:, 192 * e : 192 * (e + 1)]


def first_kernel(
    x_ref, bg, bu, bd, a_ref, act_ref, g_ref, u_ref, h_ref, wg1, wu1, wd1, wd0, wg, wu, wd, held, send, recv, local
):
    i = pl.program_id(0)
    last = pl.num_programs(0) - 1
    r, s = lax.axis_index("r"), lax.axis_index("s")
    y, c = r // 4, s % 2
    core, across, other = s + 1 - 2 * c, lax.rem(s + 2, 4), lax.rem(r + 4, 8)
    blocks = [bg.at[0], bu.at[0], bd.at[0], bg.at[1], bu.at[1], bd.at[1]]
    wholes = [wg, wu, wd, wg1, wu1, wd1]

    def copy(m, kind):
        rows = blocks[m].shape[0]
        half = rows // 2
        whole = wholes[m]

        def remote(src, dst, rr, ss):
            return pltpu.make_async_remote_copy(
                src_ref=src,
                dst_ref=dst,
                send_sem=send.at[m, kind],
                recv_sem=recv.at[m, kind],
                device_id=(0, rr, ss),
                device_id_type=MESH,
            )

        if kind == 0:
            return remote(blocks[m], whole.at[pl.ds(s * rows, rows)], r, core)
        if kind == 1:
            return remote(blocks[m].at[pl.ds(y * half, half)], whole.at[pl.ds(s * rows + y * half, half)], r, across)
        which = y if kind in (2, 3) else 1 - y
        part = whole.at[pl.ds(across * rows + which * half, half)]
        return remote(part, part, other if kind == 2 else r, s if kind == 2 else core)

    def own(m):
        rows = blocks[m].shape[0]
        return pltpu.make_async_copy(blocks[m], wholes[m].at[pl.ds(s * rows, rows)], local.at[m])

    def crossed(m):
        copy(m, 1).wait_recv()
        copy(m, 2).start()
        copy(m, 3).start()

    def turned(m):
        copy(m, 2).wait_recv()
        copy(m, 4).start()

    def arrived(m):
        own(m).wait()
        for kind in (0, 3, 4):
            copy(m, kind).wait_recv()

    @pl.when(i == 0)
    def _():
        barrier = pltpu.get_barrier_semaphore()
        for rr, ss in ((r, core), (r, across), (other, s)):
            pl.semaphore_signal(barrier, inc=1, device_id=(0, rr, ss), device_id_type=MESH)
        pl.semaphore_wait(barrier, 3)
        for m in range(6):
            copy(m, 1).start()
            own(m).start()
            if m < 3:
                copy(m, 0).start()

    x = x_ref[...]
    _, _, a = normed(x)
    a_ref[...] = a

    @pl.when(i == 0)
    def _():
        crossed(0)
        crossed(1)
        turned(0)
        turned(1)
        arrived(0)
        arrived(1)

    for k in range(3):
        cols = slice(k * 768, (k + 1) * 768)
        gate, up = nn(a, wg[:, cols]), nn(a, wu[:, cols])
        g_ref[:, cols] = gate
        u_ref[:, cols] = up
        act = (gate * lax.logistic(gate) * up).astype(bf16)
        held[:, cols] = act
        spread(act_ref, k, act)

    @pl.when(i == 0)
    def _():
        crossed(2)
        turned(2)
        arrived(2)
        pltpu.make_async_copy(wd, wd0, local.at[6]).start()
        crossed(3)
        copy(3, 0).start()

    h_ref[...] = x + nn(held[...], wd[...]).astype(bf16)

    @pl.when(i == 1)
    def _():
        crossed(4)
        copy(4, 0).start()
        turned(3)

    @pl.when(i == 2)
    def _():
        crossed(5)
        copy(5, 0).start()
        turned(4)

    @pl.when(i == 4)
    def _():
        turned(5)

    @pl.when(i == last)
    def _():
        for m in (3, 4, 5):
            arrived(m)
        pltpu.make_async_copy(wd, wd0, local.at[6]).wait()
        for m in range(6):
            for kind in range(5):
                copy(m, kind).wait_send()


def first(x, bg, bu, bd, tm=512):
    t, d = x.shape
    f = bg.shape[2]
    row = lambda n: pl.BlockSpec((tm, n), lambda i: (i, 0))
    once = lambda b: pl.BlockSpec(b.shape, lambda i: (0, 0, 0), pipeline_mode=pl.Buffered(1))
    hbm = pl.BlockSpec(memory_space=pl.ANY)
    out = jax.ShapeDtypeStruct
    return pl.pallas_call(
        first_kernel,
        grid=(t // tm,),
        in_specs=[row(d), once(bg), once(bu), once(bd)],
        out_specs=[row(d), row(f), row(f), row(f), row(d), hbm, hbm, hbm, hbm],
        out_shape=[
            out((t, d), bf16),
            out((t, f), bf16),
            out((t, f), f32),
            out((t, f), f32),
            out((t, d), bf16),
            out((d, f), bf16),
            out((d, f), bf16),
            out((f, d), bf16),
            out((f, d), bf16),
        ],
        scratch_shapes=[
            pltpu.VMEM((d, f), bf16),
            pltpu.VMEM((d, f), bf16),
            pltpu.VMEM((f, d), bf16),
            pltpu.VMEM((tm, f), bf16),
            pltpu.SemaphoreType.DMA((6, 5)),
            pltpu.SemaphoreType.DMA((6, 5)),
            pltpu.SemaphoreType.DMA((7,)),
        ],
        compiler_params=pltpu.CompilerParams(collective_id=1, has_side_effects=True, vmem_limit_bytes=62 * MIB),
        cost_estimate=pl.CostEstimate(flops=6 * t * d * f, bytes_accessed=120 * MIB, transcendentals=0),
        name="first_layer",
    )(x, bg, bu, bd)


def second_kernel(h_ref, dy_ref, g0, u0, wg, wu, wd, wd0, a_ref, act_ref, dgu_ref, dh_ref):
    f = wg.shape[1]
    h, dy = h_ref[...], dy_ref[...]
    wide, scale, a = normed(h)
    a_ref[...] = a
    by_gate = by_up = None
    for k in range(3):
        cols = slice(k * 768, (k + 1) * 768)
        gate, up = nn(a, wg[:, cols]), nn(a, wu[:, cols])
        dact = nt(dy, wd[cols, :]).astype(bf16).astype(f32)
        silu, dg, du = backward(dact, gate, up)
        spread(act_ref, k, (silu * up).astype(bf16))
        dg, du = dg.astype(bf16), du.astype(bf16)
        dgu_ref[:, k * 768 : (k + 1) * 768] = dg
        dgu_ref[:, f + k * 768 : f + (k + 1) * 768] = du
        part_gate, part_up = nt(dg, wg[:, cols]), nt(du, wu[:, cols])
        by_gate = part_gate if by_gate is None else by_gate + part_gate
        by_up = part_up if by_up is None else by_up + part_up
    da = (by_gate.astype(bf16) + by_up.astype(bf16)).astype(f32)
    along = jnp.mean(da * wide, -1, keepdims=True)
    dh = dy + (da * scale - wide * (scale * scale * scale * along)).astype(bf16)
    dh_ref[...] = dh
    for k in range(3):
        cols = slice(k * 768, (k + 1) * 768)
        dact = nt(dh, wd0[cols, :]).astype(bf16).astype(f32)
        _, dg, du = backward(dact, g0[:, cols], u0[:, cols])
        dgu_ref[:, 2 * f + k * 768 : 2 * f + (k + 1) * 768] = dg.astype(bf16)
        dgu_ref[:, 3 * f + k * 768 : 3 * f + (k + 1) * 768] = du.astype(bf16)


def second(h, dy, g0, u0, wg, wu, wd, wd0, tm=256):
    t, d = h.shape
    f = wg.shape[1]
    row = lambda n: pl.BlockSpec((tm, n), lambda i: (i, 0))
    once = lambda w: pl.BlockSpec(w.shape, lambda i: (0, 0), pipeline_mode=pl.Buffered(1))
    out = jax.ShapeDtypeStruct
    return pl.pallas_call(
        second_kernel,
        grid=(t // tm,),
        in_specs=[row(d), row(d), row(f), row(f), once(wg), once(wu), once(wd), once(wd0)],
        out_specs=[row(d), row(f), row(4 * f), row(d)],
        out_shape=[out((t, n), bf16) for n in (d, f, 4 * f, d)],
        compiler_params=pltpu.CompilerParams(vmem_limit_bytes=63 * MIB),
        cost_estimate=pl.CostEstimate(flops=12 * t * d * f, bytes_accessed=200 * MIB, transcendentals=0),
        name="second_layer",
    )(h, dy, g0, u0, wg, wu, wd, wd0)


UNITS, LAGS = 24, {"C": 2, "X": 4, "Y": 6, "Z": 8, "A": 10, "B": 12}


def sum_kernel(
    a1, dy, dh, a0, dgu, act1, act0, og, od, osq, res, tile, g, rc, kx, sx, rx, ky, sy, ry, fg, fd, sg, sd, rzg, rzd, outg, outd, square,
    csem, xsem, ysem, zsem, asem, bsem, rsem, tsem, osem,
):
    t = pl.program_id(0)
    r, s = lax.axis_index("r"), lax.axis_index("s")
    x, c, y, z = s // 2, s % 2, r // 4, r % 4
    core, across, other = s + 1 - 2 * c, lax.rem(s + 2, 4), lax.rem(r + 4, 8)
    peers = [y * 4 + lax.rem(z + k, 4) for k in (1, 2, 3)]
    down = lambda u: (u >= 9) & (u < 15)
    of_gate = lambda u: jnp.where(u < 9, u, u - 6)

    def remote(src, dst, sem, rr, ss):
        return pltpu.make_async_remote_copy(
            src_ref=src, dst_ref=dst, send_sem=sem[0], recv_sem=sem[1], device_id=(0, rr, ss), device_id_type=MESH
        )

    def pick(sem, *at):
        return sem.at[(0, *at)], sem.at[(1, *at)]

    class Kind:
        def __init__(self, u, is_down):
            self.u, self.down = u, is_down
            self.rows, self.cols = (96, 896) if is_down else (112, 512)
            self.two, self.four = lax.rem(u, 2), lax.rem(u, 4)
            self.box = (slice(None, self.rows), slice(None, self.cols))
            self.cut = (pl.ds(0, self.rows), pl.ds(0, self.cols))
            self.index = u - 9 if is_down else of_gate(u)
            self.full, self.send, self.got, self.out = (fd, sd, rzd, outd) if is_down else (fg, sg, rzg, outg)

        def c_copy(self):
            b = self.two
            everything = (slice(None), slice(None), *self.cut)
            return remote(g.at[(b, 1 - c, *everything)], rc.at[(b, *everything)], pick(csem, self.four), r, core)

        def x_copy(self):
            everything = (slice(None), *self.cut)
            return remote(
                sx.at[(self.two, *everything)], rx.at[(self.four, *everything)], pick(xsem, self.four), r, across
            )

        def y_copy(self):
            return remote(sy.at[(self.two, *self.cut)], ry.at[(self.four, *self.cut)], pick(ysem, self.four), other, s)

        def z_copies(self):
            return [
                remote(
                    self.send.at[self.two, lax.rem(z + k + 1, 4)],
                    self.got.at[self.four, k],
                    pick(zsem, self.four, k),
                    peers[k],
                    s,
                )
                for k in range(3)
            ]

        def a_copies(self):
            mine = self.out.at[self.index, y, z]
            return [remote(mine, mine, pick(asem, self.four, k), peers[k], s) for k in range(3)]

        def b_copy(self):
            mine = self.out.at[self.index, y]
            return remote(mine, mine, pick(bsem, self.four), other, s)

        def put_out(self):
            return pltpu.make_async_copy(
                self.out.at[self.index], (od if self.down else og).at[self.index], osem.at[self.u]
            )

    def both(u, work):
        here = (u >= 0) & (u < UNITS)

        @pl.when(here & jnp.logical_not(down(u)))
        def _():
            work(Kind(u, False))

        @pl.when(here & down(u))
        def _():
            work(Kind(u, True))

    def tile_copy(u, start):
        slot = lax.rem(u, 2)

        def act(copy):
            copy.start() if start else copy.wait()

        @pl.when((u < UNITS) & jnp.logical_not(down(u)))
        def _():
            first = pl.multiple_of(of_gate(u) * 512, 512)
            act(pltpu.make_async_copy(dgu.at[:, pl.ds(first, 512)], tile.at[slot, :, pl.ds(0, 512)], tsem.at[slot]))

        for source, base in ((act1, 9), (act0, 12)):

            @pl.when((u >= base) & (u < base + 3))
            def _():
                first = pl.multiple_of((u - base) * 768, 768)
                act(pltpu.make_async_copy(source.at[:, pl.ds(first, 768)], tile.at[slot], tsem.at[slot]))

    held = [pltpu.make_async_copy(src, res.at[k % 2], rsem.at[k]) for k, src in enumerate((a1, dy, dh, a0))]

    @pl.when(t == 0)
    def _():
        held[0].start()
        tile_copy(t, True)
        held[1].start()
        square[...] = jnp.zeros_like(square)
        barrier = pltpu.get_barrier_semaphore()
        for rr, ss in ((r, core), (r, across), (other, s), (peers[0], s), (peers[1], s), (peers[2], s)):
            pl.semaphore_signal(barrier, inc=1, device_id=(0, rr, ss), device_id_type=MESH)
        pl.semaphore_wait(barrier, 6)
        held[0].wait()

    def b_wait(k):
        k.b_copy().wait()
        k.put_out().start()

    def a_wait(k):
        for copy in k.a_copies():
            copy.wait()
        k.b_copy().start()

    def z_wait(k):
        for copy in k.z_copies():
            copy.wait()
        total = k.full[k.two, z]
        for i in range(3):
            total += k.got[k.four, i].astype(f32)
        rounded = total.astype(bf16)
        k.out[k.index, y, z] = rounded
        wide = rounded.astype(f32)
        wide = wide * wide
        total = square[...]
        for i in range(wide.shape[0] // 8):
            for j in range(wide.shape[1] // 128):
                total += wide[8 * i : 8 * i + 8, 128 * j : 128 * j + 128]
        square[...] = total
        for copy in k.a_copies():
            copy.start()

    def y_wait(k):
        k.y_copy().wait()
        for i in range(4):
            if k.down:
                at = (slice(24 * i, 24 * i + 24), slice(None, 896))
            else:
                at = (slice(None, 112), slice(128 * i, 128 * i + 128))
            total = ky[(k.two, *at)] + ry[(k.four, *at)].astype(f32)
            k.full[k.two, i] = total
            k.send[k.two, i] = total.astype(bf16)
        for copy in k.z_copies():
            copy.start()

    def x_wait(k):
        k.x_copy().wait()
        ky[(k.two, *k.box)] = kx[(k.two, y, *k.box)] + rx[(k.four, y, *k.box)].astype(f32)
        away = kx[(k.two, 1 - y, *k.box)] + rx[(k.four, 1 - y, *k.box)].astype(f32)
        sy[(k.two, *k.box)] = away.astype(bf16)
        k.y_copy().start()

    def c_wait(k):
        k.c_copy().wait()
        for i in range(2):
            away = g[(k.two, c, 1 - x, i, *k.box)].astype(f32) + rc[(k.two, 1 - x, i, *k.box)].astype(f32)
            sx[(k.two, i, *k.box)] = away.astype(bf16)
        k.x_copy().start()
        for i in range(2):
            kx[(k.two, i, *k.box)] = g[(k.two, c, x, i, *k.box)].astype(f32) + rc[(k.two, x, i, *k.box)].astype(f32)

    both(t - LAGS["B"], b_wait)
    both(t - LAGS["A"], a_wait)
    both(t - LAGS["Z"], z_wait)
    both(t - LAGS["Y"], y_wait)
    both(t - LAGS["X"], x_wait)
    both(t - LAGS["C"], c_wait)
    both(t - 1, lambda k: k.c_copy().start())

    for k, when in ((1, 9), (2, 12), (3, 15)):

        @pl.when(t == when)
        def _():
            held[k].wait()
            if k < 3:
                held[k + 1].start()

    def store(k, product):
        for block in range(4):
            for half in range(2):
                first = (2 * block + half) * k.rows
                g[(k.two, block % 2, block // 2, half, *k.box)] = product[first : first + k.rows].astype(bf16)

    @pl.when(t < UNITS)
    def _():
        tile_copy(t, False)
        tile_copy(t + 1, True)
        slot = lax.rem(t, 2)

        @pl.when(jnp.logical_not(down(t)))
        def _():
            store(Kind(t, False), tn(res[jnp.where(t < 9, 0, 1)], tile[slot, :, :512]))

        @pl.when(down(t))
        def _():
            store(Kind(t, True), tn(tile[slot], res[jnp.where(t < 12, 1, 0)]))

    @pl.when(t == pl.num_programs(0) - 1)
    def _():
        osq[...] = square[...]
        for u in range(UNITS):
            Kind(u, 9 <= u < 15).put_out().wait()


def summed(a1, dy, dh, a0, dgu, act1, act0):
    t, d = a1.shape
    hbm = pl.BlockSpec(memory_space=pl.ANY)
    out, vmem, dma = jax.ShapeDtypeStruct, pltpu.VMEM, pltpu.SemaphoreType.DMA
    og, od = (18, 2, 4, 112, 128), (6, 2, 4, 24, 896)
    part = (112, 896)
    return pl.pallas_call(
        sum_kernel,
        grid=(UNITS + LAGS["B"],),
        in_specs=[hbm] * 7,
        out_specs=[hbm, hbm, pl.BlockSpec((8, 128), lambda i: (0, 0))],
        out_shape=[out(og, bf16), out(od, bf16), out((8, 128), f32)],
        scratch_shapes=[
            vmem((2, t, d), bf16),
            vmem((2, t, 768), bf16),
            vmem((2, 2, 2, 2, *part), bf16),
            vmem((2, 2, 2, *part), bf16),
            vmem((2, 2, *part), f32),
            vmem((2, 2, *part), bf16),
            vmem((4, 2, *part), bf16),
            vmem((2, *part), f32),
            vmem((2, *part), bf16),
            vmem((4, *part), bf16),
            vmem((2, *og[2:]), f32),
            vmem((2, *od[2:]), f32),
            vmem((2, *og[2:]), bf16),
            vmem((2, *od[2:]), bf16),
            vmem((4, 3, *og[3:]), bf16),
            vmem((4, 3, *od[3:]), bf16),
            vmem(og, bf16),
            vmem(od, bf16),
            vmem((8, 128), f32),
            dma((2, 4)),
            dma((2, 4)),
            dma((2, 4)),
            dma((2, 4, 3)),
            dma((2, 4, 3)),
            dma((2, 4)),
            dma((4,)),
            dma((2,)),
            dma((UNITS,)),
        ],
        compiler_params=pltpu.CompilerParams(collective_id=2, has_side_effects=True, vmem_limit_bytes=63 * MIB),
        name="sums",
    )(a1, dy, dh, a0, dgu, act1, act0)


def adamw(w, m, v, g):
    m = 0.9 * m + 0.1 * g
    v = 0.95 * v + 0.05 * g * g
    step = m * lax.rsqrt(v + 1e-8) + 0.1 * w
    return (w - 0.02 * step).astype(bf16), m, v


def solution(mesh):
    def step(x, dy, wg, wu, wd, *state):
        x, dy = x[0], dy[0]
        a0, act0, g0, u0, h, wg1, wu1, wd1, wd0 = first(x, wg, wu, wd)
        a1, act1, dgu, dh = second(h, dy, g0, u0, wg1, wu1, wd1, wd0)
        og, od, squares = summed(a1, dy, dh, a0, dgu, act1, act0)
        squares = lax.psum(jnp.sum(squares), ("r", "s"))
        gu = og.reshape(2, 9, 2, 4, 112, 128).transpose(0, 2, 4, 1, 3, 5).reshape(2, *wg.shape[1:2], 2, wg.shape[2])
        gate, up = gu[::-1, :, 0], gu[::-1, :, 1]
        dn = od.reshape(wd.shape)[::-1]
        gradients = [g.astype(f32) for g in (gate, up, dn)]
        count = 4 * sum(g.size for g in gradients)
        factor = jnp.minimum(1.0, 0.5 * lax.rsqrt(squares / count + 1e-30))
        new = [
            adamw(w.astype(f32), m, v, g * factor)
            for w, m, v, g in zip((wg, wu, wd), state[:3], state[3:], gradients, strict=True)
        ]
        return tuple(one[which] for which in range(3) for one in new)

    states, cut = P(("rep", "r", "s"), None, None), P(None, "s", None)
    return jax.shard_map(
        step,
        mesh=mesh,
        in_specs=(states, states) + (cut,) * 9,
        out_specs=(P("rep", "s", None),) * 9,
        check_vma=False,
    )
```

time: 921 us -> 581 us (0.63)
  Pallas kernels: 0 us -> 479 us
  matrix products: 475 us -> 0 us
  waiting for transfers between devices: 337 us -> 0 us
  blocking collectives: 6.35 us -> 41.2 us
  between operations: 17 us -> 1.37 us
  local copies, waits for them, and re-layouts: 37.7 us -> 27.5 us
  other arithmetic: 41.8 us -> 31.7 us
    pallas_call x0 -> x3, Pallas kernels: none -> 479 us  [the longest x1 193 us: summed(): pl.pallas_call(sum_kernel, grid=(UNITS + LAGS['B'],), in_specs=[hbm] * 7,...]
    dot_general x15 -> x0, matrix products: 475 us -> none  [the longest x5 173 us: layer(): up = jnp.dot(a, w['w_up'], preferred_element_type=jnp.float32)]
    psum x1 -> x0, waiting for transfers between devices: 213 us -> none  [summed(): lax.psum(lax.psum_scatter(term, 's', scatter_dimension=0, tiled=True), 'r')]
    reduce_scatter x6 -> x0, waiting for transfers between devices: 85.6 us -> none  [summed(): lax.psum_scatter(term, 's', scatter_dimension=0, tiled=True)]
    all_gather x6 -> x0, waiting for transfers between devices: 36.7 us -> none  [fetched(): lax.all_gather(w[number], 's', axis=0, tiled=True)]
    psum x1, blocking collectives: 6.35 us -> 41.2 us  [step(): squares = lax.psum(jnp.sum(squares), ('r', 's'))]
    unnamed x36 -> x9, local copies, waits for them, and re-layouts: 30.1 us -> 3.12 us
    reshape x0 -> x2, local copies, waits for them, and re-layouts: none -> 14.8 us  [step(): og.reshape(2, 9, 2, 4, 112, 128).transpose(0, 2, 4, 1, 3, 5)]
  transfers between devices with their start and end apart: 13 -> 0, of which waited for: 8 -> 0; matrix products, arithmetic and copies ran while one was open for 41% -> 0% of each run, Pallas kernels for 0% -> 0%
where the time goes in v1:
time: 581 us
  Pallas kernels  479 us (82%)
  blocking collectives  41.2 us (7%)
  other arithmetic  31.7 us (5%)
  local copies, waits for them, and re-layouts  27.5 us (5%)
    pallas_call x1, Pallas kernels, summed(): pl.pallas_call(sum_kernel, grid=(UNITS + LAGS['B'],), in_specs=[hbm] * 7,...  193 us
    pallas_call x1, Pallas kernels, second(): pl.pallas_call(second_kernel, grid=(t // tm,), in_specs=[row(d), row(d),...  151 us
    pallas_call x1, Pallas kernels, first(): pl.pallas_call(first_kernel, grid=(t // tm,), in_specs=[row(d), once(bg),...  135 us
    psum x1, blocking collectives, step(): squares = lax.psum(jnp.sum(squares), ('r', 's'))  41.2 us
    convert_element_type x2, other arithmetic, adamw(): return ((w - 0.02 * step).astype(bf16), m, v)  22.1 us
    reshape x2, local copies, waits for them, and re-layouts, step(): og.reshape(2, 9, 2, 4, 112, 128).transpose(0, 2, 4, 1, 3, 5)  14.8 us

profile of v1, /device:TPU:0, one launch (start us, length us, event | category | flops | bytes accessed | tf_op | source)
XLA Modules:
  0.0 580.8 jit_solution(12412384414161751759)
XLA Ops:
  0.6 134.9 %first_layer.1 = (bf16[4096,896]{1,0:T(8,128)(2,1)}, bf16[4096,2304]{1,0:T(8,128)(2,1)}, f32[4096,2304]{1,0:T(8,128)}, f32[4096,2304]{1,0:T(8,128)}, bf16[4096,8...) custom-call(bf16[4096,896]{1,0:T(8,128)(2,1)} %bitcast.26, ...), custom_call_target="tpu_custom_call" | custom-call | flops 50734301184 | bytes 125829120 | tf_op jit(solution)/shard_map/first_layer/pallas_call | solution.py:175
  135.6 150.7 %second_layer.1 = (bf16[4096,896]{1,0:T(8,128)(2,1)}, bf16[4096,2304]{1,0:T(8,128)(2,1)}, bf16[4096,9216]{1,0:T(8,128)(2,1)}, bf16[4096,896]{1,0:T(8,128)(2,1)}) custom-call(bf16[4096,896]{1,0:T(8,128)(2,1)} %get-tuple-element.25.h_ref, bf16[4096,896]{1,0:T(8,128)(2,1)} %bitcast.22, f32[4096,2304]{1,0:T(8,128)} %get-tuple-element.26.g0, ...), custom_call_target="tpu_custom_call" | custom-call | flops 101468602368 | bytes 209715200 | tf_op jit(solution)/shard_map/second_layer/pallas_call | solution.py:242
  286.3 193.3 %sums.1 = (bf16[18,2,4,112,128]{4,3,2,1,0:T(8,128)(2,1)}, bf16[6,2,4,24,896]{4,3,2,1,0:T(8,128)(2,1)}, f32[8,128]{1,0:T(8,128)}) custom-call(bf16[4096,896]{1,0:T(8,128)(2,1)} %get-tuple-element.32.a1, bf16[4096,896]{1,0:T(8,128)(2,1)} %bitcast.23, bf16[4096,896]{1,0:T(8,128)(2,1)} %get-tuple-element.33.dh, bf16[4096,896]{1,0:T(8,128)(2,1)} %get-tuple-element.34.a0, ...), custom_call_target="tpu_custom_call" | custom-call | tf_op jit(solution)/shard_map/sums/pallas_call | solution.py:474
  479.6 1.3 reduce_sum.9
  480.9 41.2 %psum.7 = f32[]{:T(128)} all-reduce(f32[]{:T(128)} %reduce_sum.9), channel_id=1, replica_groups=mesh['rep'=1,'r'=8,'s'=4] {'r','s'}, use_global_device_ids=true, to_apply=%region_1.0 | all-reduce | flops 1 | bytes 8 | tf_op jit(solution)/shard_map/psum | solution.py:528
  522.8 5.7 copy.30
  528.5 9.1 %reshape.34 = bf16[2,224,2,2304]{3,2,1,0:T(2,128)(2,1)} reshape(bf16[2,2,112,9,4,128]{5,4,3,2,1,0:T(4,128)(2,1)} %bitcast.21) | data formatting | bytes 8257536 | tf_op jit(solution)/shard_map/reshape | solution.py:529
  537.6 9.6 %fusion.19 = (bf16[2,224,1,2304]{3,2,1,0:T(2,128)(2,1)}, bf16[2,224,1,2304]{3,2,1,0:T(2,128)(2,1)S(1)}) fusion(bf16[2,224,2,2304]{3,2,1,0:T(2,128)(2,1)} %reshape.34), kind=kLoop, calls=%fused_computation.30 | loop fusion | bytes 8257536 | tf_op jit(solution)/shard_map/slice | solution.py:530
  547.2 8.4 %convert_multiply_fusion.4 = f32[2,224,1,2304]{3,2,1,0:T(1,128)} fusion(bf16[2,224,1,2304]{3,2,1,0:T(2,128)(2,1)} %get-tuple-element.50, f32[]{:T(128)S(6)} %min_shard_map.3), kind=kLoop, calls=%fused_computation.28 | loop fusion | flops 2064384 | bytes 6193156 | tf_op jit(solution)/shard_map/mul | solution.py:536
  555.6 0.0 copy-start.1
  555.6 0.0 copy-start.2
  555.6 0.2 copy.24
  555.8 1.9 copy-done.1
  557.8 0.7 copy-done.2
  558.4 0.0 copy-start
  558.4 0.0 copy-start.3
  558.4 7.2 %fusion.8 = (bf16[2,576,896]{2,1,0:T(8,128)(2,1)}, f32[2,576,896]{2,1,0:T(8,128)}, f32[2,576,896]{2,1,0:T(8,128)}) fusion(bf16[2,576,896]{2,1,0:T(8,128)(2,1)S(1)} %copy-done.2, f32[]{:T(128)S(6)} %min_shard_map.3, bf16[2,576,896]{2,1,0:T(8,128)(2,1)} %bitcast.25, f32[2,576,896]{2,1,0:T(8,128)S(1)} %copy-done.1, f32[2,576,896]{2,1,0:T(8,128)} %param.18), kind=kLoop, calls=%fused_computation.17 | loop fusion | flops 17547264 | bytes 22708228 | tf_op jit(solution)/shard_map/convert_element_type | solution.py:519
  565.6 0.0 copy-done
  565.6 0.3 copy-done.3
  565.9 14.9 %fusion.2 = (bf16[2,224,2304]{2,1,0:T(8,128)(2,1)}, f32[2,224,2304]{2,1,0:T(8,128)}, f32[2,224,2304]{2,1,0:T(8,128)}, bf16[2,224,2304]{2,1,0:T(8,128)(2,1)}, f32...) fusion(bf16[2,224,2304]{2,1,0:T(8,128)(2,1)S(1)} %copy-done.3, f32[]{:T(128)S(6)} %min_shard_map.3, ...), kind=kLoop, calls=%fused_computation.11 | loop fusion | flops 33030144 | bytes 47480836 | tf_op jit(solution)/shard_map/convert_element_type | solution.py:519
Async XLA Ops:
  555.6 2.2 copy-start.1
  555.6 2.8 copy-start.2
  558.4 7.2 %copy-start = (f32[2,224,1,2304]{3,2,1,0:T(1,128)S(1)}, f32[2,224,1,2304]{3,2,1,0:T(1,128)}, u32[]{:S(2)}) copy-start(f32[2,224,1,2304]{3,2,1,0:T(1,128)} %convert_multiply_fusion.4) | copy-start | bytes 12386308
  558.4 7.5 %copy-start.3 = (bf16[2,224,2304]{2,1,0:T(8,128)(2,1)S(1)}, bf16[2,224,2304]{2,1,0:T(8,128)(2,1)}, u32[]{:S(2)}) copy-start(bf16[2,224,2304]{2,1,0:T(8,128)(2,1)} %bg.1) | copy-start | bytes 6193156
